TPU v7x, 32 devices: a whole 2x2x4 slice. The times are simulated.
32 devices in a mesh: section: 2 (over core), dp: 2 (over y), tensor: 8 (over z, x).
Axes of the slice: x: 2, y: 2, z: 4, core: 2. Of those that a mesh axis runs over, the one named last changes fastest.
Arguments:
- residual_parts: bfloat16 [2, 768, 16384], P('section', 'dp', 'tensor'), may hold values from -120 to 120
- attn_out: bfloat16 [2, 768, 16384], P('section', 'dp', 'tensor'), may hold values from -6 to 6
- ffn_input: bfloat16 [2, 768, 53248], P('section', 'dp', 'tensor'), may hold values from -6 to 6
- norm_gain: float32 [2, 16384], P('section', 'tensor'), may hold values from 0.25 to 1.75
- mixing: bfloat16 [2, 52, 52], P('section'), may hold values from -0.875 to 0.875
- blocks: int32 [2, 2], P('section'), may hold values from 0 to 25, as said below
Outputs:
- hess_in: float32 [2, 16384, 1024], P('section', 'tensor', 'dp')
- hess_o: float32 [2, 16384, 1024], P('section', 'tensor', 'dp')
- hess_down: float32 [2, 2048, 2048], P('section', 'tensor', 'dp')
Inputs may be any that keep to these rules, and one draw needn't show every extreme that they name: `blocks`: entry [s, 0] is below 16; entry [s, 1] is below 26. In every draw one layer has entry [s, 0] = 0 and entry [s, 1] = 25.
All inputs are finite; a program needn't handle non-finite values.
Results may differ from a plain program's by a relative error of at most 0.0038.
Values may be sent and summed in bfloat16 or wider, within the bound.
A program may use at most 128 MiB of HBM per device.

v0:
```python
import math
import jax
import jax.numpy as jnp
from jax import lax
from jax.sharding import PartitionSpec as P

D = 16384
KB = 52
HBLK = 1024
BLK = 2048
EPS = 1e-05


def passed_along(x, axis, by):
    devices = lax.axis_size(axis)
    pairs = [(i, i + by) for i in range(devices) if 0 <= i + by < devices]
    return lax.ppermute(x, axis, pairs)


def broadcast(value, axis, source):
    kept = jnp.where(lax.axis_index(axis) == source, value, 0).astype(value.dtype)
    return lax.psum(kept, axis)


def bit_parity(values):
    total = jnp.zeros_like(values)
    for position in range(16):
        total = total + values // (1 << position) % 2
    return total % 2


def sylvester(order):
    index = jnp.arange(order, dtype=jnp.int32)
    parity = bit_parity(jnp.bitwise_and(index[:, None], index[None, :]))
    return (1 - 2 * parity).astype(jnp.float32)


def gram(left, right):
    return lax.dot_general(
        left, right, (((0,), (0,)), ((), ())), preferred_element_type=jnp.float32
    )


def local(residual_parts, attn_out, ffn_input, norm_gain, mixing, blocks):
    local_d = residual_parts.shape[2]
    local_f = ffn_input.shape[2]
    token_rows = residual_parts.shape[1]
    own_part = residual_parts[0]
    earlier = passed_along(own_part, "section", 1)
    layer_in = earlier.astype(jnp.float32) + own_part.astype(jnp.float32)
    square_total = lax.psum(jnp.sum(layer_in * layer_in, axis=1), "tensor")
    normed = (layer_in * lax.rsqrt(square_total / D + EPS)[:, None] * norm_gain[0][None, :]).astype(
        jnp.bfloat16
    )
    attention = attn_out[0]
    first_col = blocks[0, 0] * HBLK
    width = min(HBLK, local_d)
    offset = first_col % local_d
    norm_slab = lax.dynamic_slice_in_dim(normed, offset, width, 1)
    attn_slab = lax.dynamic_slice_in_dim(attention, offset, width, 1)
    norm_list, attn_list = ([], [])
    owner = first_col // local_d + 0
    norm_got = broadcast(norm_slab, "tensor", owner)
    attn_got = broadcast(attn_slab, "tensor", owner)
    norm_list.append(norm_got)
    attn_list.append(attn_got)
    norm_block = norm_list[0]
    attn_block = attn_list[0]
    tensor_count = lax.axis_size("tensor")
    member = lax.axis_index("tensor")
    a_local = local_f // KB
    order_a = a_local * tensor_count
    cube = ffn_input[0].reshape(token_rows, a_local, KB)
    mixed = jnp.einsum("rak,kc->rac", cube, mixing[0], preferred_element_type=jnp.float32)
    turned = jnp.einsum("rac,ae->rec", mixed, sylvester(a_local), precision=lax.Precision.HIGHEST)
    turned = turned.reshape(token_rows, local_f)
    start = blocks[0, 1] * BLK
    doubled = jnp.concatenate([turned, turned], axis=1)
    window = lax.dynamic_slice_in_dim(doubled, start % local_f, BLK, 1)
    target = (start + jnp.arange(BLK, dtype=jnp.int32)) // local_f
    parity = bit_parity(jnp.bitwise_and(target, member))
    signs = (1 - 2 * parity).astype(jnp.float32) / math.sqrt(order_a)
    term = window * signs[None, :]
    share = BLK // tensor_count
    rotated = lax.psum(term, "tensor").astype(jnp.bfloat16)
    own_cols = lax.dynamic_slice_in_dim(rotated, member * share, share, 1)
    part_in = gram(normed, norm_block)
    part_o = gram(attention, attn_block)
    part_down = gram(own_cols, rotated)
    summed = (
        lax.psum_scatter(part_in, "dp", scatter_dimension=1, tiled=True),
        lax.psum_scatter(part_o, "dp", scatter_dimension=1, tiled=True),
        lax.psum_scatter(part_down, "dp", scatter_dimension=1, tiled=True),
    )
    scale = 2.0 / (token_rows * lax.axis_size("dp"))
    hess_in = (scale * summed[0])[None]
    hess_o = (scale * summed[1])[None]
    hess_down = (scale * summed[2])[None]
    return (hess_in, hess_o, hess_down)


def solution(mesh):
    return jax.shard_map(
        local,
        mesh=mesh,
        in_specs=(
            P("section", "dp", "tensor"),
            P("section", "dp", "tensor"),
            P("section", "dp", "tensor"),
            P("section", "tensor"),
            P("section", None, None),
            P("section", None),
        ),
        out_specs=(
            P("section", "tensor", "dp"),
            P("section", "tensor", "dp"),
            P("section", "tensor", "dp"),
        ),
        check_vma=False,
    )
```

profile of v0, /device:TPU:0, one launch (start us, length us, event | category | flops | bytes accessed | tf_op | source)
XLA Modules:
  0.0 523.9 jit_solution(5240815388376950331)
XLA Ops:
  8.1 3.6 collective-permute-start
  11.7 7.8 %copy.11 = bf16[1,384,6656]{1,2,0:T(8,128)(2,1)} copy(bf16[1,384,6656]{2,1,0:T(8,128)(2,1)} %param.8) | data formatting | bytes 10223616 | tf_op args[2]
  19.4 8.1 %reshape_squeeze.3 = bf16[384,128,52]{0,2,1:T(8,128)(2,1)} reshape(bf16[1,384,6656]{1,2,0:T(8,128)(2,1)} %copy.11) | data formatting | bytes 10223616 | tf_op jit(solution)/shard_map/reshape;squeeze | solution.py:73
  27.5 8.4 %fusion.156 = f32[384,128,52]{0,2,1:T(8,128)} fusion(bf16[384,128,52]{0,2,1:T(8,128)(2,1)} %reshape_squeeze.3, bf16[1,52,52]{2,1,0:T(8,128)(2,1)S(1)} %copy-done), kind=kOutput, calls=%fused_computation.259 | convolution fusion | flops 265814016 | bytes 15340832 | tf_op jit(solution)/shard_map/rak,kc->rac/dot_general | solution.py:74
  35.9 0.6 fusion.253
  37.8 15.9 %fusion.2 = f32[384,128,52]{0,1,2:T(8,128)S(1)} fusion(f32[384,128,52]{0,2,1:T(8,128)} %fusion.156), kind=kOutput, calls=%fused_computation.7 | convolution fusion | flops 3931668480 | bytes 20447232 | tf_op jit(solution)/shard_map/rac,ae->rec/dot_general | solution.py:75
  53.7 10.1 %copy.12 = f32[384,128,52]{0,2,1:T(8,128)} copy(f32[384,128,52]{0,1,2:T(8,128)S(1)} %fusion.2) | data formatting | bytes 20447232 | tf_op jit(solution)/shard_map/rac,ae->rec/transpose | solution.py:75
  63.8 11.5 %reshape.392 = f32[384,6656]{0,1:T(8,128)} reshape(f32[384,128,52]{0,2,1:T(8,128)} %copy.12) | data formatting | bytes 20447232 | tf_op jit(solution)/shard_map/reshape | solution.py:76
  75.5 2.9 fusion.6
  78.4 2.5 select_bitcast_fusion
  80.8 2.5 multiply_reduce_fusion
  83.3 129.9 %all-reduce.6 = (f32[384]{0:T(512)S(1)}, bf16[384,2048]{0,1:T(8,128)(2,1)}) all-reduce(f32[384]{0:T(512)S(1)} %multiply_reduce_fusion, f32[384,2048]{0,1:T(8,128)S(1)} %fusion.6), channel_id=1, replica_groups=mesh['section'=2,'dp'=2,'tensor'=8] {'tensor'}, use_global_device_ids=true, to_apply=%region_1.0 | all-reduce | flops 786816 | bytes 4721664 | tf_op jit(solution)/shard_map/psum | solution.py:51
  213.2 2.6 multiply_convert_fusion
  215.8 1.3 dynamic-slice_select_fusion
  217.2 3.7 fusion.8
  221.2 83.6 %all-reduce.5.cloned.1.call-done = (bf16[384,1024]{1,0:T(8,128)(2,1)}, bf16[384,1024]{1,0:T(8,128)(2,1)}) async-done(((bf16[384,1024]{1,0:T(8,128)(2,1)}, bf16[384,1024]{1,0:T(8,128)(2,1)}), (bf16[384,1024]{1,0:T(8,128)(2,1)}, bf16[384,1024]{1,0:T(8,128)(2,1)})) %all-reduce.5.cloned.1.call-update) | async-done | bytes 1572880 | tf_op jit(solution)/shard_map/psum | solution.py:22
  304.8 6.7 %convolution_bitcast_fusion = f32[2048,1024]{1,0:T(8,128)} fusion(bf16[384,1024]{1,0:T(8,128)(2,1)} %get-tuple-element.6, bf16[1,384,2048]{2,1,0:T(8,128)(2,1)S(1)} %copy-done.2), kind=kOutput, calls=%fused_computation.4 | convolution fusion | flops 1610612736 | bytes 10747904 | tf_op jit(solution)/shard_map/dot_general | solution.py:39
  311.6 1.1 copy-done.3
  312.6 5.9 %fusion.254 = f32[2048,1024]{1,0:T(8,128)} fusion(bf16[384,2048]{1,0:T(8,128)(2,1)S(1)} %multiply_convert_fusion, bf16[384,1024]{1,0:T(8,128)(2,1)S(1)} %copy-done.3), kind=kOutput, calls=%fused_computation.458 | convolution fusion | flops 1610612736 | bytes 10747904 | tf_op jit(solution)/shard_map/dot_general | solution.py:39
  318.6 2.3 multiply_bitcast_fusion.2
  320.9 89.2 %reduce-scatter.6.cloned.1.call-done = f32[2048,512]{1,0:T(8,128)} async-done(((f32[2048,1024]{1,0:T(8,128)}), f32[2048,512]{1,0:T(8,128)}) %reduce-scatter.6.cloned.1.call-update) | async-done | bytes 4194320 | tf_op jit(solution)/shard_map/reduce_scatter | solution.py:92
  410.1 4.7 multiply_bitcast_fusion
  414.8 96.7 %reduce-scatter.4.cloned.1.call-done = f32[2048,512]{1,0:T(8,128)} async-done(((f32[2048,1024]{1,0:T(8,128)}), f32[2048,512]{1,0:T(8,128)}) %reduce-scatter.4.cloned.1.call-update) | async-done | bytes 4194320 | tf_op jit(solution)/shard_map/reduce_scatter | solution.py:91
  511.6 4.7 multiply_bitcast_fusion.1
  (23 shorter events, 0.7 us)
Async XLA Ops:
  8.0 19.5 %copy-start = (bf16[1,52,52]{2,1,0:T(8,128)(2,1)S(1)}, bf16[1,52,52]{2,1,0:T(8,128)(2,1)}, u32[]{:S(2)}) copy-start(bf16[1,52,52]{2,1,0:T(8,128)(2,1)} %param.10) | copy-start | bytes 16228
  8.0 296.7 %all-reduce.5.cloned.1.call-start = ((), (), s32[]{:S(2)}) async-start(), calls=%async_computation.6 | async-start | bytes 3145728 | tf_op jit(solution)/shard_map/psum | solution.py:22
  8.1 72.8 %collective-permute-start = (bf16[384,2048]{1,0:T(8,128)(2,1)}, bf16[384,2048]{1,0:T(8,128)(2,1)}, u32[]{:S(2)}, u32[]{:S(2)}) collective-permute-start(bf16[384,2048]{1,0:T(8,128)(2,1)} %bitcast.37), channel_id=1, source_target_pairs={{0,16},{1,17},{2,18},{3,19},{4,20},{5,21},{6,22},{7,23},{8,24},{9,... | collective-permute-start | bytes 4718600 | tf_op jit(solution)/shard_map/ppermute | solution.py:17
  27.5 8.4 %copy-start.5 = (s32[1,2]{1,0:T(1,128)S(1)}, s32[1,2]{1,0:T(1,128)}, u32[]{:S(2)}) copy-start(s32[1,2]{1,0:T(1,128)} %param.11) | copy-start | bytes 28
  80.8 132.4 %copy-start.4 = (f32[1,2048]{1,0:T(1,128)S(1)}, f32[1,2048]{1,0:T(1,128)}, u32[]{:S(2)}) copy-start(f32[1,2048]{1,0:T(1,128)} %param.9) | copy-start | bytes 24580
  217.1 87.6 %copy-start.2 = (bf16[1,384,2048]{2,1,0:T(8,128)(2,1)S(1)}, bf16[1,384,2048]{2,1,0:T(8,128)(2,1)}, u32[]{:S(2)}) copy-start(bf16[1,384,2048]{2,1,0:T(8,128)(2,1)} %param.7) | copy-start | bytes 4718596
  217.2 101.4 %reduce-scatter.8.cloned.1.call-start = ((), (), s32[]{:S(2)}) async-start(), calls=%async_computation.5 | async-start | bytes 3145728 | tf_op jit(solution)/shard_map/reduce_scatter | solution.py:93
  220.9 189.2 %reduce-scatter.6.cloned.1.call-start = ((), (), s32[]{:S(2)}) async-start(), calls=%async_computation.4 | async-start | bytes 12582912 | tf_op jit(solution)/shard_map/reduce_scatter | solution.py:92
  311.5 1.1 copy-start.3
  311.5 200.0 %reduce-scatter.4.cloned.1.call-start = ((), (), s32[]{:S(2)}) async-start(), calls=%async_computation.3 | async-start | bytes 12582912 | tf_op jit(solution)/shard_map/reduce_scatter | solution.py:91
  410.1 106.2 %copy-start.1 = (bf16[1,52,52]{2,1,0:T(8,128)(2,1)S(1)}, bf16[1,52,52]{2,1,0:T(8,128)(2,1)}, u32[]{:S(2)}) copy-start(bf16[1,52,52]{2,1,0:T(8,128)(2,1)} %param.10) | copy-start | bytes 16228
Sparse Core Ops, SparseCore 0:
  217.3 87.4 all-reduce.4
Sparse Core Ops, SparseCore 1:
  221.0 29.9 reduce-scatter.7
  311.6 98.4 reduce-scatter.5
  412.3 99.2 reduce-scatter.3
where the time goes:
time: 525 us; the launch traced here: 524 us
  waiting for transfers between devices  270 us (51%)
  blocking collectives  130 us (25%)
  matrix products  40.5 us (8%)
  local copies, waits for them, and re-layouts  39.2 us (7%)
  other arithmetic  23.6 us (4%)
  between operations  17.1 us (3%)
    psum x1, blocking collectives, local(): square_total = lax.psum(jnp.sum(layer_in * layer_in, axis=1), 'tensor')  130 us
    reduce_scatter x1, waiting for transfers between devices, local(): lax.psum_scatter(part_in, 'dp', scatter_dimension=1, tiled=True)  96.7 us
    reduce_scatter x1, waiting for transfers between devices, local(): lax.psum_scatter(part_o, 'dp', scatter_dimension=1, tiled=True)  89.2 us
    psum x1, waiting for transfers between devices, broadcast(): return lax.psum(kept, axis)  83.6 us
    dot_general x3, matrix products, gram(): lax.dot_general(left, right, (((0,), (0,)), ((), ())), preferred_element_...  16.3 us
    dot_general x1, matrix products, local(): jnp.einsum('rac,ae->rec', mixed, sylvester(a_local), precision=lax.Precis...  15.9 us
    reshape x1, local copies, waits for them, and re-layouts, local(): turned = turned.reshape(token_rows, local_f)  11.5 us
  transfers between devices with their start and end apart: 5, of which 3 were waited for; matrix products, arithmetic and copies ran while one was open for 17% of the time, Pallas kernels for 0%

commit v1 on v0

--- a/solution.py
+++ b/solution.py
@@ -11,6 +11,11 @@
 EPS = 1e-05
 
 
+def use_ends(chunk, row_axis):
+    out_arr = jnp.sum(jax.lax.all_gather(chunk, axis_name=row_axis), 0)
+    return out_arr
+
+
 def passed_along(x, axis, by):
     devices = lax.axis_size(axis)
     pairs = [(i, i + by) for i in range(devices) if 0 <= i + by < devices]
@@ -19,7 +24,7 @@
 
 def broadcast(value, axis, source):
     kept = jnp.where(lax.axis_index(axis) == source, value, 0).astype(value.dtype)
-    return lax.psum(kept, axis)
+    return use_ends(kept, axis)
 
 
 def bit_parity(values):

time: 525 us -> 473 us (0.901)
  waiting for transfers between devices: 270 us -> 206 us
  other arithmetic: 23.6 us -> 32 us
    psum x1 -> x0, waiting for transfers between devices: 83.6 us -> none  [broadcast(): return lax.psum(kept, axis)]
    all_gather x0 -> x2, waiting for transfers between devices: none -> 83.4 us  [use_ends(): out_arr = jnp.sum(jax.lax.all_gather(chunk, axis_name=row_axis), 0)]
    reduce_scatter x1, waiting for transfers between devices: 89.2 us -> 25.4 us  [local(): lax.psum_scatter(part_o, 'dp', scatter_dimension=1, tiled=True)]
    reduce_sum x0 -> x2, other arithmetic: none -> 8.61 us  [use_ends(): out_arr = jnp.sum(jax.lax.all_gather(chunk, axis_name=row_axis), 0)]
  transfers between devices with their start and end apart: 5 -> 6, of which waited for: 3 -> 3; matrix products, arithmetic and copies ran while one was open for 17% -> 22% of each run, Pallas kernels for 0% -> 0%
where the time goes in v1:
time: 473 us; the launch traced here: 472 us
  waiting for transfers between devices  206 us (44%)
  blocking collectives  135 us (29%)
  matrix products  39.3 us (8%)
  local copies, waits for them, and re-layouts  38.9 us (8%)
  other arithmetic  32 us (7%)
  between operations  17.1 us (4%)
    psum x1, blocking collectives, local(): square_total = lax.psum(jnp.sum(layer_in * layer_in, axis=1), 'tensor')  135 us
    reduce_scatter x1, waiting for transfers between devices, local(): lax.psum_scatter(part_in, 'dp', scatter_dimension=1, tiled=True)  96.7 us
    all_gather x2, waiting for transfers between devices, use_ends(): out_arr = jnp.sum(jax.lax.all_gather(chunk, axis_name=row_axis), 0)  83.4 us
    reduce_scatter x1, waiting for transfers between devices, local(): lax.psum_scatter(part_o, 'dp', scatter_dimension=1, tiled=True)  25.4 us
    dot_general x1, matrix products, local(): jnp.einsum('rac,ae->rec', mixed, sylvester(a_local), precision=lax.Precis...  15.9 us
    dot_general x3, matrix products, gram(): lax.dot_general(left, right, (((0,), (0,)), ((), ())), preferred_element_...  15 us
    reshape x1, local copies, waits for them, and re-layouts, local(): turned = turned.reshape(token_rows, local_f)  11.6 us
    transpose x1, local copies, waits for them, and re-layouts, local(): jnp.einsum('rac,ae->rec', mixed, sylvester(a_local), precision=lax.Precis...  10.1 us
  transfers between devices with their start and end apart: 6, of which 3 were waited for; matrix products, arithmetic and copies ran while one was open for 22% of the time, Pallas kernels for 0%

profile of v1, /device:TPU:0, one launch (start us, length us, event | category | flops | bytes accessed | tf_op | source)
XLA Modules:
  0.0 471.6 jit_solution(5819857293900433226)
XLA Ops:
  8.1 1.3 fusion.253
  10.1 2.4 dynamic-slice_select_fusion
  12.6 3.5 collective-permute-start
  16.1 7.8 %copy.14 = bf16[1,384,6656]{1,2,0:T(8,128)(2,1)} copy(bf16[1,384,6656]{2,1,0:T(8,128)(2,1)} %param.8) | data formatting | bytes 10223616 | tf_op args[2]
  23.9 8.1 %reshape_squeeze.3 = bf16[384,128,52]{0,2,1:T(8,128)(2,1)} reshape(bf16[1,384,6656]{1,2,0:T(8,128)(2,1)} %copy.14) | data formatting | bytes 10223616 | tf_op jit(solution)/shard_map/reshape;squeeze | solution.py:78
  32.0 8.4 %fusion.156 = f32[384,128,52]{0,2,1:T(8,128)} fusion(bf16[384,128,52]{0,2,1:T(8,128)(2,1)} %reshape_squeeze.3, bf16[1,52,52]{2,1,0:T(8,128)(2,1)S(1)} %copy-done), kind=kOutput, calls=%fused_computation.259 | convolution fusion | flops 265814016 | bytes 15340832 | tf_op jit(solution)/shard_map/rak,kc->rac/dot_general | solution.py:79
  41.0 15.9 %fusion.2 = f32[384,128,52]{0,1,2:T(8,128)S(1)} fusion(f32[384,128,52]{0,2,1:T(8,128)} %fusion.156), kind=kOutput, calls=%fused_computation.7 | convolution fusion | flops 3931668480 | bytes 20447232 | tf_op jit(solution)/shard_map/rac,ae->rec/dot_general | solution.py:80
  56.9 10.1 %copy.17 = f32[384,128,52]{0,2,1:T(8,128)} copy(f32[384,128,52]{0,1,2:T(8,128)S(1)} %fusion.2) | data formatting | bytes 20447232 | tf_op jit(solution)/shard_map/rac,ae->rec/transpose | solution.py:80
  67.1 11.6 %reshape.389 = f32[384,6656]{0,1:T(8,128)} reshape(f32[384,128,52]{0,2,1:T(8,128)} %copy.17) | data formatting | bytes 20447232 | tf_op jit(solution)/shard_map/reshape | solution.py:81
  78.8 3.0 fusion.6
  81.8 2.0 multiply_reduce_fusion
  83.8 134.7 %all-reduce.2 = (f32[384]{0:T(512)S(1)}, bf16[384,2048]{0,1:T(8,128)(2,1)}) all-reduce(f32[384]{0:T(512)S(1)} %multiply_reduce_fusion, f32[384,2048]{0,1:T(8,128)S(1)} %fusion.6), channel_id=1, replica_groups=mesh['section'=2,'dp'=2,'tensor'=8] {'tensor'}, use_global_device_ids=true, to_apply=%region_1.0 | all-reduce | flops 786816 | bytes 4721664 | tf_op jit(solution)/shard_map/psum | solution.py:56
  218.5 2.7 multiply_convert_fusion
  222.6 2.1 fusion.8
  225.0 4.3 reduce_sum.35
  229.3 7.4 %convolution_bitcast_fusion = f32[2048,1024]{1,0:T(8,128)} fusion(bf16[384,1024]{1,0:T(8,128)(2,1)S(1)} %reduce_sum.35, bf16[1,384,2048]{2,1,0:T(8,128)(2,1)} %param.7), kind=kOutput, calls=%fused_computation.4 | convolution fusion | flops 1610612736 | bytes 10747904 | tf_op jit(solution)/shard_map/dot_general | solution.py:44
  236.7 83.3 %all-gather.6.cloned.1.call-done = bf16[3072,1024]{1,0:T(8,128)(2,1)} async-done(((bf16[384,1024]{1,0:T(8,128)(2,1)}), bf16[3072,1024]{1,0:T(8,128)(2,1)}) %all-gather.6.cloned.1.call-update) | async-done | bytes 6291472 | tf_op jit(solution)/shard_map/all_gather | solution.py:15
  320.1 4.3 reduce_sum.34
  324.4 5.6 %fusion.254 = f32[2048,1024]{1,0:T(8,128)} fusion(bf16[384,2048]{1,0:T(8,128)(2,1)S(1)} %multiply_convert_fusion, bf16[384,1024]{1,0:T(8,128)(2,1)S(1)} %reduce_sum.34), kind=kOutput, calls=%fused_computation.458 | convolution fusion | flops 1610612736 | bytes 10747904 | tf_op jit(solution)/shard_map/dot_general | solution.py:44
  330.0 2.4 multiply_bitcast_fusion.2
  332.4 25.4 %reduce-scatter.6.cloned.1.call-done = f32[2048,512]{1,0:T(8,128)} async-done(((f32[2048,1024]{1,0:T(8,128)}), f32[2048,512]{1,0:T(8,128)}) %reduce-scatter.6.cloned.1.call-update) | async-done | bytes 4194320 | tf_op jit(solution)/shard_map/reduce_scatter | solution.py:97
  357.8 4.7 %multiply_bitcast_fusion = f32[1,2048,512]{2,1,0:T(8,128)} fusion(f32[2048,512]{1,0:T(8,128)} %reduce-scatter.6.cloned.1.call-done), kind=kLoop, calls=%fused_computation.5 | loop fusion | flops 1048576 | bytes 8388608 | tf_op jit(solution)/shard_map/broadcast_in_dim | solution.py:102
  362.6 96.7 %reduce-scatter.4.cloned.1.call-done = f32[2048,512]{1,0:T(8,128)} async-done(((f32[2048,1024]{1,0:T(8,128)}), f32[2048,512]{1,0:T(8,128)}) %reduce-scatter.4.cloned.1.call-update) | async-done | bytes 4194320 | tf_op jit(solution)/shard_map/reduce_scatter | solution.py:96
  459.3 4.7 multiply_bitcast_fusion.1
  (26 shorter events, 2.0 us)
Async XLA Ops:
  8.0 24.0 %copy-start = (bf16[1,52,52]{2,1,0:T(8,128)(2,1)S(1)}, bf16[1,52,52]{2,1,0:T(8,128)(2,1)}, u32[]{:S(2)}) copy-start(bf16[1,52,52]{2,1,0:T(8,128)(2,1)} %param.10) | copy-start | bytes 16228
  8.0 217.0 %all-gather.4.cloned.1.call-start = ((), (), s32[]{:S(2)}) async-start(), calls=%async_computation.4 | async-start | bytes 7077888 | tf_op jit(solution)/shard_map/all_gather | solution.py:15
  12.5 307.5 %all-gather.6.cloned.1.call-start = ((), (), s32[]{:S(2)}) async-start(), calls=%async_computation.7 | async-start | bytes 7077888 | tf_op jit(solution)/shard_map/all_gather | solution.py:15
  12.6 69.2 %collective-permute-start = (bf16[384,2048]{1,0:T(8,128)(2,1)}, bf16[384,2048]{1,0:T(8,128)(2,1)}, u32[]{:S(2)}, u32[]{:S(2)}) collective-permute-start(bf16[384,2048]{1,0:T(8,128)(2,1)} %bitcast.38), channel_id=1, source_target_pairs={{0,16},{1,17},{2,18},{3,19},{4,20},{5,21},{6,22},{7,23},{8,24},{9,... | collective-permute-start | bytes 4718600 | tf_op jit(solution)/shard_map/ppermute | solution.py:22
  78.8 3.0 copy-start.2
  81.7 136.7 %copy-start.4 = (f32[1,2048]{1,0:T(1,128)S(1)}, f32[1,2048]{1,0:T(1,128)}, u32[]{:S(2)}) copy-start(f32[1,2048]{1,0:T(1,128)} %param.9) | copy-start | bytes 24580
  218.5 4.1 copy-start.3
  222.5 107.5 %reduce-scatter.8.cloned.1.call-start = ((), (), s32[]{:S(2)}) async-start(), calls=%async_computation.6 | async-start | bytes 3145728 | tf_op jit(solution)/shard_map/reduce_scatter | solution.py:98
  224.7 133.2 %reduce-scatter.6.cloned.1.call-start = ((), (), s32[]{:S(2)}) async-start(), calls=%async_computation.5 | async-start | bytes 12582912 | tf_op jit(solution)/shard_map/reduce_scatter | solution.py:97
  236.7 222.6 %reduce-scatter.4.cloned.1.call-start = ((), (), s32[]{:S(2)}) async-start(), calls=%async_computation.3 | async-start | bytes 12582912 | tf_op jit(solution)/shard_map/reduce_scatter | solution.py:96
  357.8 106.2 %copy-start.1 = (bf16[1,52,52]{2,1,0:T(8,128)(2,1)S(1)}, bf16[1,52,52]{2,1,0:T(8,128)(2,1)}, u32[]{:S(2)}) copy-start(bf16[1,52,52]{2,1,0:T(8,128)(2,1)} %param.10) | copy-start | bytes 16228
Sparse Core Ops, SparseCore 0:
  12.7 122.4 all-gather.3
  222.6 97.3 all-gather.5
Sparse Core Ops, SparseCore 1:
  225.8 30.5 reduce-scatter.7
  258.5 99.2 reduce-scatter.5
  360.0 99.2 reduce-scatter.3
